TPU v7x, 256 devices: a whole 4x4x8 slice. The times are simulated.
256 devices in a mesh: pop: 64 (over x, z, core), mp: 4 (over y).
Axes of the slice: x: 4, y: 4, z: 8, core: 2. Of those that a mesh axis runs over, the one named last changes fastest.
Arguments:
- tokens: bfloat16 [256, 3584], replicated, may hold values from -60 to 60
- target: bfloat16 [256, 3584], P(None, 'mp'), may hold values from -6 to 6
- w_query: bfloat16 [3584, 3584], P('pop', 'mp'), may hold values from -0.09375 to 0.09375
- w_key: bfloat16 [3584, 512], P(None, 'mp'), may hold values from -0.09375 to 0.09375
- w_value: bfloat16 [3584, 512], P(None, 'mp'), may hold values from -0.09375 to 0.09375
- w_out: bfloat16 [3584, 3584], P('mp', 'pop'), may hold values from -0.09375 to 0.09375
- query_left_factors: bfloat16 [64, 3584, 4], P('pop'), may hold values from -0.09375 to 0.09375
- query_right_factors: bfloat16 [64, 4, 3584], P('pop', None, 'mp'), may hold values from -6 to 6
- o_left: bfloat16 [64, 3584, 4], P('pop', 'mp'), may hold values from -0.09375 to 0.09375
- o_right: bfloat16 [64, 4, 3584], P('pop'), may hold values from -6 to 6
- member_ids: int32 [64], P('pop'), may hold values from 0 to 63, each once
Outputs:
- grad_query: float32 [3584, 3584], P('pop', 'mp')
- grad_out: float32 [3584, 3584], P('mp', 'pop')
- fitness: float32 [64], P('pop')
Inputs may be any that keep to these rules, and one draw needn't show every extreme that they name: `member_ids`: every number from 0 to 63 appears once.
All inputs are finite; a program needn't handle non-finite values.
Results may differ from a plain program's by a relative error of at most 0.005.
Values may be sent and summed in bfloat16 or wider, within the bound.
No kernel may reach another device: no remote copies, remote signals or barrier semaphores. Data moves between devices by JAX's collectives and lax.ppermute only.
A program may use at most 64 MiB of HBM per device.

v0:
```python
import math
import jax
import jax.numpy as jnp
from jax import lax
from jax.sharding import Mesh
from jax.sharding import PartitionSpec as P

D = 3584
HEADS = 28
KV_HEADS = 4
HEAD_DIM = 128
RANK = 4
POP = ("pop_0", "pop_1", "pop_2")
noise_scale = 0.5
rope_base = 1000000.0
spread_floor = 0.001


def in_order(parts, dim):
    parts = jnp.moveaxis(parts, 0, dim)
    shape = parts.shape
    return parts.reshape(*shape[:dim], shape[dim] * shape[dim + 1], *shape[dim + 2 :])


def all_blocks(shard, axes, turns):
    parts = shard[None]
    for k in turns:
        parts = lax.all_gather(parts, axes[k], axis=0, tiled=True)
    held = [lax.axis_size(axes[k]) for k in reversed(turns)]
    parts = parts.reshape(*held, *shard.shape)
    turned = sorted(range(len(turns)), key=lambda place: turns[len(turns) - 1 - place])
    return parts.transpose(*turned, *range(len(turns), parts.ndim)).reshape(-1, *shard.shape)


def whole_of(shard, axes, turns, dim):
    return in_order(all_blocks(shard, axes, turns), dim)


def cut_along(shard, dim, devices):
    before, after = (shard.shape[:dim], shard.shape[dim + 1 :])
    return jnp.moveaxis(shard.reshape(*before, devices, -1, *after), dim, 0)


def summed_on_arrival(shard, axis, dim):
    devices = lax.axis_size(axis)
    parts = lax.all_to_all(cut_along(shard, dim, devices), axis, 0, 0, tiled=True)
    return jnp.sum(parts.astype(jnp.float32), axis=0)


def copy_for_each(shard, axis):
    copies = jnp.broadcast_to(shard, (lax.axis_size(axis), *shard.shape))
    return lax.all_to_all(copies, axis, split_axis=0, concat_axis=0, tiled=True)


def of_everyone(shard, axis):
    return copy_for_each(shard, axis).sum(axis=0)


def gathered_copies(shard, axis, dim):
    return in_order(copy_for_each(shard, axis), dim)


def side_by_side(arrays, axis, dim, along):
    columns = [a.reshape(*a.shape[:along], -1) for a in arrays]
    both = jnp.concatenate(columns, axis=along)
    result, at, done = (lax.all_gather(both, axis, axis=dim, tiled=True), 0, [])
    for a, column in zip(arrays, columns):
        share = result[..., at : at + column.shape[along]]
        done.append(share.reshape(*share.shape[:along], *a.shape[along:]))
        at += column.shape[along]
    return tuple(done)


def tables(count, head_size):
    position = jnp.arange(count, dtype=jnp.float32)
    index = jnp.arange(head_size // 2, dtype=jnp.float32)
    freq = jnp.exp(-math.log(rope_base) * 2.0 * index / head_size)
    angle = position[:, None] * freq[None, :]
    return (jnp.cos(angle)[:, None, :], jnp.sin(angle)[:, None, :])


def rotate(field, cosine_table, sine):
    half = field.shape[-1] // 2
    first = field[..., :half]
    second = field[..., half:]
    return jnp.concatenate(
        [first * cosine_table - second * sine, second * cosine_table + first * sine], axis=-1
    )


def per_device(
    tokens,
    target,
    w_query,
    w_key,
    w_value,
    w_out,
    query_left_factors,
    query_right_factors,
    o_left,
    o_right,
    member_ids,
):
    tok = tokens.shape[0]
    local_feats = w_query.shape[1]
    local_kv = w_key.shape[1] // HEAD_DIM
    group = HEADS // KV_HEADS
    local_heads = local_kv * group
    slots = query_left_factors.shape[0]
    scale = HEAD_DIM ** (-0.5)
    cosine_table, sine = tables(tok, HEAD_DIM)
    base = jnp.dot(tokens, whole_of(w_query, POP, (0, 1, 2), 0), preferred_element_type=jnp.float32)
    keys = rotate(
        jnp.dot(tokens, w_key, preferred_element_type=jnp.float32).reshape(tok, local_kv, HEAD_DIM),
        cosine_table,
        sine,
    ).astype(jnp.bfloat16)
    values = (
        jnp.dot(tokens, w_value, preferred_element_type=jnp.float32)
        .astype(jnp.bfloat16)
        .reshape(tok, local_kv, HEAD_DIM)
    )
    signs = (1 - 2 * (member_ids % 2)).astype(jnp.float32)
    factor = noise_scale * signs[:, None, None]
    lowrank_product = jnp.einsum(
        "td,mdr->mtr", tokens, query_left_factors, preferred_element_type=jnp.float32
    ).astype(jnp.bfloat16)
    query = base[None] + factor * jnp.einsum(
        "olj,ojv->olv", lowrank_product, query_right_factors, preferred_element_type=jnp.float32
    )
    query = rotate(
        query.reshape(slots, tok, local_heads, HEAD_DIM), cosine_table[None], sine[None]
    ).astype(jnp.bfloat16)
    query = query.reshape(slots, tok, local_kv, group, HEAD_DIM)
    scores = jnp.einsum("mtkgd,skd->mkgts", query, keys, preferred_element_type=jnp.float32) * scale
    causal = jnp.arange(tok)[:, None] >= jnp.arange(tok)[None, :]
    scores = jnp.where(causal, scores, -1e30)
    probs = jax.nn.softmax(scores, axis=-1).astype(jnp.bfloat16)
    mixed = (
        jnp.einsum("mkgts,skd->mtkgd", probs, values, preferred_element_type=jnp.float32)
        .astype(jnp.bfloat16)
        .reshape(slots, tok, local_feats)
    )
    low_out = jnp.einsum("mtf,mfr->mtr", mixed, o_left, preferred_element_type=jnp.float32)
    right_full = o_right.astype(jnp.float32)
    part = jnp.einsum(
        "mtf,fe->mte",
        mixed,
        lax.all_gather(w_out, POP, axis=1, tiled=True),
        preferred_element_type=jnp.float32,
    )
    term = part + factor * jnp.einsum(
        "mtr,mre->mte", low_out, right_full, precision=lax.Precision.HIGHEST
    )
    output = summed_on_arrival(term.astype(jnp.bfloat16), "mp", 2)
    diff = output - target.astype(jnp.float32)[None]
    errors = of_everyone(jnp.sum(diff * diff, axis=(1, 2)), "mp")
    fitness = -(errors / (tok * D))
    count = slots * lax.axis_size(POP)
    everyone = gathered_copies(fitness, POP, 0)
    mean = jnp.sum(everyone) / count
    spread = jnp.sum((everyone - mean) * (everyone - mean)) / count
    weight = signs * (fitness - mean) / jnp.sqrt(spread + spread_floor)
    every_weight = gathered_copies(weight, POP, 0)
    right_factors_gathered, left_all = side_by_side((query_right_factors, o_left), POP, 0, 1)
    rows_q = lax.all_to_all(query_left_factors, POP, split_axis=1, concat_axis=0, tiled=True)
    cols_o = lax.all_to_all(o_right, POP, split_axis=2, concat_axis=0, tiled=True)
    whole_population = rows_q.shape[0]
    left_q = jnp.transpose(
        rows_q.astype(jnp.float32) * every_weight[:, None, None], (1, 0, 2)
    ).reshape(rows_q.shape[1], whole_population * RANK)
    right_q = right_factors_gathered.astype(jnp.float32).reshape(
        whole_population * RANK, local_feats
    )
    grad_query = jnp.dot(left_q, right_q, precision=lax.Precision.HIGHEST) / noise_scale
    output_left_factor = jnp.transpose(
        left_all.astype(jnp.float32) * every_weight[:, None, None], (1, 0, 2)
    ).reshape(local_feats, whole_population * RANK)
    right_o = cols_o.astype(jnp.float32).reshape(whole_population * RANK, cols_o.shape[2])
    grad_out = jnp.dot(output_left_factor, right_o, precision=lax.Precision.HIGHEST) / noise_scale
    return (grad_query, grad_out, fitness)


def solution(mesh):
    torus = Mesh(mesh.devices.reshape(4, 8, 2, mesh.shape["mp"]), ("pop_0", "pop_1", "pop_2", "mp"))
    placed = (
        P(),
        P(None, "mp"),
        P(POP, "mp"),
        P(None, "mp"),
        P(None, "mp"),
        P("mp", POP),
        P(POP, None, None),
        P(POP, None, "mp"),
        P(POP, "mp", None),
        P(POP, None, None),
        P(POP),
    )
    return jax.shard_map(
        per_device,
        mesh=torus,
        in_specs=placed,
        out_specs=(P(POP, "mp"), P("mp", POP), P(POP)),
        check_vma=False,
    )
```

profile of v0, /device:TPU:1, one launch (start us, length us, event | category | flops | bytes accessed | tf_op | source)
XLA Modules:
  0.0 428.7 jit_solution(7784847421207332163)
XLA Ops:
  7.2 13.0 %all-gather = bf16[224,896]{1,0:T(8,128)(2,1)} all-gather(bf16[56,896]{1,0:T(8,128)(2,1)} %param.13), channel_id=2, replica_groups=mesh['pop_0'=4,'pop_1'=8,'pop_2'=2,'mp'=4] {'pop_0'}, dimensions={0}, use_global_device_ids=true | all-gather | bytes 501760 | tf_op jit(solution)/shard_map/all_gather | solution.py:28
  20.3 49.6 %all-gather.6.cloned.1.call-done = bf16[32,56,896]{2,1,0:T(8,128)(2,1)} async-done(((bf16[4,56,896]{2,1,0:T(8,128)(2,1)}), bf16[32,56,896]{2,1,0:T(8,128)(2,1)}) %all-gather.6.cloned.1.call-update) | async-done | bytes 3211280 | tf_op jit(solution)/shard_map/all_gather | solution.py:28
  70.0 0.7 all-gather.10.cloned.1.call-update
  71.4 0.7 convolution_bitcast_fusion
  72.2 1.0 fusion.18
  73.1 0.5 fusion.13
  73.6 19.9 %all-gather.8.cloned.1.call-done = bf16[64,56,896]{2,1,0:T(8,128)(2,1)} async-done(((bf16[32,56,896]{2,1,0:T(8,128)(2,1)}), bf16[64,56,896]{2,1,0:T(8,128)(2,1)}) %all-gather.8.cloned.1.call-update) | async-done | bytes 6422544 | tf_op jit(solution)/shard_map/all_gather | solution.py:28
  93.5 3.3 copy.114
  96.9 2.1 fusion.29
  99.1 2.1 fusion.3
  101.1 1.5 copy.115
  102.6 0.9 fusion.27
  103.5 1.3 copy.140
  104.8 1.3 copy.141
  106.1 1.4 fusion.7
  107.5 0.6 fusion.28
  108.2 1.2 copy-done.2
  109.4 0.3 fusion.2
  109.7 0.3 copy-done.13
  110.0 2.6 convolution_convert_fusion
  112.6 0.2 fusion.23
  112.8 65.1 %all-gather.10.cloned.1.call-done = bf16[896,3584]{0,1:T(8,128)(2,1)} async-done(((bf16[896,56]{0,1:T(8,128)(2,1)}), bf16[896,3584]{0,1:T(8,128)(2,1)}) %all-gather.10.cloned.1.call-update) | async-done | bytes 6422544 | tf_op jit(solution)/shard_map/all_gather | solution.py:149
  177.9 4.9 %fusion.30 = f32[256,3584]{1,0:T(8,128)S(1)} fusion(bf16[256,896]{0,1:T(8,128)(2,1)S(1)} %bitcast.106, bf16[896,3584]{0,1:T(8,128)(2,1)} %all-gather.10.cloned.1.call-done), kind=kOutput, calls=%fused_computation.58 | convolution fusion | flops 1644167168 | bytes 10551296 | tf_op jit(solution)/shard_map/mtf,fe->mte/dot_general | solution.py:146
  182.8 3.1 fusion.1
  185.9 3.3 reshape.288
  189.2 1.5 copy.145
  190.7 4.0 all-to-all-start.1
  194.7 0.2 copy.126
  194.9 0.3 reshape.291
  195.3 22.5 %all-to-all-done.1 = bf16[4,1,256,896]{3,2,1,0:T(8,128)(2,1)S(1)} async-done(((bf16[4,1,256,896]{3,2,1,0:T(8,128)(2,1)}), bf16[4,1,256,896]{3,2,1,0:T(8,128)(2,1)S(1)}, u32[]{:S(2)}, u32[]{:S(2)}) %all-to-all-start.1) | async-done | bytes 1835040 | tf_op jit(solution)/shard_map/all_to_all | solution.py:46
  217.8 0.2 convert_reduce_fusion
  218.1 0.9 multiply_reduce_fusion
  218.9 0.6 broadcast_in_dim.34
  219.6 6.5 %all_to_all.47 = f32[4,1,1]{2,1,0:T(1,128)S(1)} all-to-all(f32[4,1,1]{2,1,0:T(1,128)S(1)} %broadcast_in_dim.34), channel_id=1, replica_groups=mesh['pop_0'=4,'pop_1'=8,'pop_2'=2,'mp'=4] {'mp'}, dimensions={0} | all-to-all | bytes 32 | tf_op jit(solution)/shard_map/all_to_all | solution.py:52
  226.0 0.6 reduce_sum.57
  227.3 0.6 broadcast_in_dim.35
  227.9 7.9 %all-to-all-start.3 = ((f32[64,1,1]{2,1,0:T(1,128)}), f32[64,1,1]{2,1,0:T(1,128)S(1)}, u32[]{:S(2)}, u32[]{:S(2)}) async-start(f32[64,1,1]{2,1,0:T(1,128)} %broadcast_in_dim.35), calls=%async_computation.3 | async-start | bytes 65536 | tf_op jit(solution)/shard_map/all_to_all | solution.py:52
  235.9 51.8 %all-gather.1 = bf16[64,1,7168]{2,1,0:T(2,128)(2,1)S(1)} all-gather(bf16[1,1,7168]{2,1,0:T(2,128)(2,1)S(1)} %maximum_bitcast_fusion.2), channel_id=1, replica_groups=mesh['pop_0'=4,'pop_1'=8,'pop_2'=2,'mp'=4] {'pop_0','pop_1','pop_2'}, dimensions={0}, use_global_device_ids=true | all-gather | bytes 931840 | tf_op jit(solution)/shard_map/all_gather | solution.py:66
  287.7 3.2 copy.129
  290.9 1.2 copy.146
  292.2 7.3 %all-to-all-start.5 = ((bf16[1,4,3584]{1,0,2:T(2,128)(2,1)}), bf16[1,4,3584]{1,0,2:T(2,128)(2,1)S(1)}, u32[]{:S(2)}, u32[]{:S(2)}) async-start(bf16[1,4,3584]{1,0,2:T(2,128)(2,1)} %copy.129), calls=%async_computation.5 | async-start | bytes 3670016 | tf_op jit(solution)/shard_map/all_to_all | solution.py:167
  299.4 2.0 slice_convert_fusion
  301.5 3.2 copy.112
  304.7 0.7 reduce_sum.58
  306.1 38.7 %all-to-all-done.5 = bf16[1,4,3584]{1,0,2:T(2,128)(2,1)S(1)} async-done(((bf16[1,4,3584]{1,0,2:T(2,128)(2,1)}), bf16[1,4,3584]{1,0,2:T(2,128)(2,1)S(1)}, u32[]{:S(2)}, u32[]{:S(2)}) %all-to-all-start.5) | async-done | bytes 28704 | tf_op jit(solution)/shard_map/all_to_all | solution.py:167
  344.8 6.2 %all-to-all-start = ((bf16[1,3584,4]{2,0,1:T(2,128)(2,1)}), bf16[1,3584,4]{2,0,1:T(2,128)(2,1)}, u32[]{:S(2)}, u32[]{:S(2)}) async-start(bf16[1,3584,4]{2,0,1:T(2,128)(2,1)} %copy.112), calls=%async_computation | async-start | bytes 3670016 | tf_op jit(solution)/shard_map/all_to_all | solution.py:166
  351.0 0.6 multiply_reduce_fusion.1
  352.3 44.0 %all-to-all-done = bf16[1,3584,4]{2,0,1:T(2,128)(2,1)} async-done(((bf16[1,3584,4]{2,0,1:T(2,128)(2,1)}), bf16[1,3584,4]{2,0,1:T(2,128)(2,1)}, u32[]{:S(2)}, u32[]{:S(2)}) %all-to-all-start) | async-done | bytes 28704 | tf_op jit(solution)/shard_map/all_to_all | solution.py:166
  396.3 0.6 broadcast_in_dim.36
  396.9 6.0 %all-to-all-start.4 = ((f32[64,1,1]{2,1,0:T(1,128)}), f32[64,1,1]{2,1,0:T(1,128)S(1)}, u32[]{:S(2)}, u32[]{:S(2)}) async-start(f32[64,1,1]{2,1,0:T(1,128)} %broadcast_in_dim.36), calls=%async_computation.4 | async-start | bytes 65536 | tf_op jit(solution)/shard_map/all_to_all | solution.py:52
  403.0 1.8 copy.127
  404.7 1.3 reshape.292
  406.0 1.8 copy.130
  407.9 0.1 all_to_all.39
  408.1 3.7 copy.113
  411.8 0.1 reshape.295
  412.0 0.2 all-to-all-done.4
  412.2 0.6 reduce.10
  412.8 1.6 multiply_bitcast_fusion
  414.4 2.8 copy.128
  417.2 1.5 reshape.293
  418.8 0.1 copy.125
  418.9 1.1 convolution_multiply_fusion.3
  420.0 1.1 convolution_multiply_fusion.2
  (39 shorter events, 0.5 us)
Async XLA Ops:
  7.2 64.2 %copy-start = (bf16[256,3584]{1,0:T(8,128)(2,1)S(1)}, bf16[256,3584]{1,0:T(8,128)(2,1)}, u32[]{:S(2)}) copy-start(bf16[256,3584]{1,0:T(8,128)(2,1)} %param.11) | copy-start | bytes 5505028
  7.2 62.7 %all-gather.6.cloned.1.call-start = ((), (), s32[]{:S(2)}) async-start(), calls=%async_computation.6 | async-start | bytes 3612672 | tf_op jit(solution)/shard_map/all_gather | solution.py:28
  20.2 51.2 %copy-start.4 = (bf16[3584,128]{1,0:T(8,128)(2,1)S(1)}, bf16[3584,128]{1,0:T(8,128)(2,1)}, u32[]{:S(2)}) copy-start(bf16[3584,128]{1,0:T(8,128)(2,1)} %param.14) | copy-start | bytes 2752516
  20.3 73.3 %all-gather.8.cloned.1.call-start = ((), (), s32[]{:S(2)}) async-start(), calls=%async_computation.7 | async-start | bytes 9633792 | tf_op jit(solution)/shard_map/all_gather | solution.py:28
  69.9 107.9 %all-gather.10.cloned.1.call-start = ((), (), s32[]{:S(2)}) async-start(), calls=%async_computation.8 | async-start | bytes 6522880 | tf_op jit(solution)/shard_map/all_gather | solution.py:149
  96.9 2.2 copy-start.9
  96.9 2.2 copy-start.11
  106.1 1.4 copy-start.6
  106.1 1.4 copy-start.7
  108.1 1.3 copy-start.2
  108.2 1.9 copy-start.13
  110.0 2.6 copy-start.12
  112.8 70.0 %copy-start.8 = (bf16[1,4,3584]{2,1,0:T(4,128)(2,1)S(1)}, bf16[1,4,3584]{2,1,0:T(4,128)(2,1)}, u32[]{:S(2)}) copy-start(bf16[1,4,3584]{2,1,0:T(4,128)(2,1)} %param.20) | copy-start | bytes 86020
  190.7 27.1 %all-to-all-start.1 = ((bf16[4,1,256,896]{3,2,1,0:T(8,128)(2,1)}), bf16[4,1,256,896]{3,2,1,0:T(8,128)(2,1)S(1)}, u32[]{:S(2)}, u32[]{:S(2)}) async-start(bf16[4,1,256,896]{3,2,1,0:T(8,128)(2,1)} %bitcast.98), calls=%async_computation.1 | async-start | bytes 3670016 | tf_op jit(solution)/shard_map/all_to_all | solution.py:46
  194.7 23.3 %copy-start.5 = (bf16[256,896]{1,0:T(8,128)(2,1)S(1)}, bf16[256,896]{1,0:T(8,128)(2,1)}, u32[]{:S(2)}) copy-start(bf16[256,896]{1,0:T(8,128)(2,1)} %param.12) | copy-start | bytes 1376260
  227.9 64.2 %all-to-all-start.3 = ((f32[64,1,1]{2,1,0:T(1,128)}), f32[64,1,1]{2,1,0:T(1,128)S(1)}, u32[]{:S(2)}, u32[]{:S(2)}) async-start(f32[64,1,1]{2,1,0:T(1,128)} %broadcast_in_dim.35), calls=%async_computation.3 | async-start | bytes 65536 | tf_op jit(solution)/shard_map/all_to_all | solution.py:52
  292.2 52.6 %all-to-all-start.5 = ((bf16[1,4,3584]{1,0,2:T(2,128)(2,1)}), bf16[1,4,3584]{1,0,2:T(2,128)(2,1)S(1)}, u32[]{:S(2)}, u32[]{:S(2)}) async-start(bf16[1,4,3584]{1,0,2:T(2,128)(2,1)} %copy.129), calls=%async_computation.5 | async-start | bytes 3670016 | tf_op jit(solution)/shard_map/all_to_all | solution.py:167
  299.4 2.1 copy-start.10
  344.8 51.5 %all-to-all-start = ((bf16[1,3584,4]{2,0,1:T(2,128)(2,1)}), bf16[1,3584,4]{2,0,1:T(2,128)(2,1)}, u32[]{:S(2)}, u32[]{:S(2)}) async-start(bf16[1,3584,4]{2,0,1:T(2,128)(2,1)} %copy.112), calls=%async_computation | async-start | bytes 3670016 | tf_op jit(solution)/shard_map/all_to_all | solution.py:166
  396.9 15.3 %all-to-all-start.4 = ((f32[64,1,1]{2,1,0:T(1,128)}), f32[64,1,1]{2,1,0:T(1,128)S(1)}, u32[]{:S(2)}, u32[]{:S(2)}) async-start(f32[64,1,1]{2,1,0:T(1,128)} %broadcast_in_dim.36), calls=%async_computation.4 | async-start | bytes 65536 | tf_op jit(solution)/shard_map/all_to_all | solution.py:52
  407.9 4.9 %copy-start.3 = (f32[64,3584]{0,1:T(8,128)S(1)}, f32[64,3584]{0,1:T(8,128)}, u32[]{:S(2)}) copy-start(f32[64,3584]{0,1:T(8,128)} %copy.127) | copy-start | bytes 2752516
  414.3 6.7 %copy-start.1 = (bf16[256,3584]{1,0:T(8,128)(2,1)S(1)}, bf16[256,3584]{1,0:T(8,128)(2,1)}, u32[]{:S(2)}) copy-start(bf16[256,3584]{1,0:T(8,128)(2,1)} %param.11) | copy-start | bytes 5505028
Sparse Core Ops, SparseCore 0:
  20.4 49.4 all-gather.5
  71.7 21.7 all-gather.7
  96.2 81.5 all-gather.9
where the time goes:
time: 430 us; the launch traced here: 429 us
  waiting for transfers between devices  241 us (56%)
  blocking collectives  71.3 us (17%)
  local copies, waits for them, and re-layouts  38.2 us (9%)
  starting transfers between devices  31.5 us (7%)
  matrix products  18.6 us (4%)
  between operations  17.9 us (4%)
  other arithmetic  10.5 us (2%)
    all_gather x2, waiting for transfers between devices, all_blocks(): parts = lax.all_gather(parts, axes[k], axis=0, tiled=True)  69.5 us
    all_gather x1, waiting for transfers between devices, per_device(): lax.all_gather(w_out, POP, axis=1, tiled=True)  65.1 us
    all_gather x1, blocking collectives, side_by_side(): result, at, done = (lax.all_gather(both, axis, axis=dim, tiled=True), 0, [])  51.8 us
    all_to_all x1, waiting for transfers between devices, per_device(): lax.all_to_all(query_left_factors, POP, split_axis=1, concat_axis=0, tile...  44 us
    all_to_all x1, waiting for transfers between devices, per_device(): lax.all_to_all(o_right, POP, split_axis=2, concat_axis=0, tiled=True)  38.7 us
    all_to_all x1, waiting for transfers between devices, summed_on_arrival(): lax.all_to_all(cut_along(shard, dim, devices), axis, 0, 0, tiled=True)  22.5 us
    all_to_all x2, starting transfers between devices, copy_for_each(): return lax.all_to_all(copies, axis, split_axis=0, concat_axis=0, tiled=True)  14 us
    all_gather x1, blocking collectives, all_blocks(): parts = lax.all_gather(parts, axes[k], axis=0, tiled=True)  13 us
  transfers between devices with their start and end apart: 8, of which 7 were waited for; matrix products, arithmetic and copies ran while one was open for 9% of the time, Pallas kernels for 0%

commit v1 on v0

--- a/solution.py
+++ b/solution.py
@@ -25,7 +25,9 @@
 def all_blocks(shard, axes, turns):
     parts = shard[None]
     for k in turns:
-        parts = lax.all_gather(parts, axes[k], axis=0, tiled=True)
+        parts = jnp.concatenate(
+            lax.all_to_all(jnp.stack([parts] * lax.axis_size(axes[k])), axes[k], 0, 0), axis=0
+        )
     held = [lax.axis_size(axes[k]) for k in reversed(turns)]
     parts = parts.reshape(*held, *shard.shape)
     turned = sorted(range(len(turns)), key=lambda place: turns[len(turns) - 1 - place])

time: 430 us -> 404 us (0.940)
  waiting for transfers between devices: 241 us -> 194 us
  blocking collectives: 71.3 us -> 81.4 us
  starting transfers between devices: 31.5 us -> 39.2 us
    all_to_all x0 -> x1, waiting for transfers between devices: none -> 87.4 us  [all_blocks(): lax.all_to_all(jnp.stack([parts] * lax.axis_size(axes[k])), axes[k], 0, 0)]
    all_gather x2 -> x0, waiting for transfers between devices: 69.5 us -> none  [all_blocks(): parts = lax.all_gather(parts, axes[k], axis=0, tiled=True)]
    all_gather x1, waiting for transfers between devices: 65.1 us -> 0.01 us  [per_device(): lax.all_gather(w_out, POP, axis=1, tiled=True)]
    all_to_all x0 -> x2, blocking collectives: none -> 22.9 us  [all_blocks(): lax.all_to_all(jnp.stack([parts] * lax.axis_size(axes[k])), axes[k], 0, 0)]
    all_gather x1 -> x0, blocking collectives: 13 us -> none  [all_blocks(): parts = lax.all_gather(parts, axes[k], axis=0, tiled=True)]
    all_to_all x0 -> x1, starting transfers between devices: none -> 8.31 us  [all_blocks(): lax.all_to_all(jnp.stack([parts] * lax.axis_size(axes[k])), axes[k], 0, 0)]
  transfers between devices with their start and end apart: 8 -> 7, of which waited for: 7 -> 5; matrix products, arithmetic and copies ran while one was open for 9% -> 11% of each run, Pallas kernels for 0% -> 0%
where the time goes in v1:
time: 404 us; the launch traced here: 403 us
  waiting for transfers between devices  194 us (48%)
  blocking collectives  81.4 us (20%)
  starting transfers between devices  39.2 us (10%)
  local copies, waits for them, and re-layouts  36.8 us (9%)
  matrix products  19.5 us (5%)
  between operations  18.2 us (5%)
  other arithmetic  14 us (3%)
    all_to_all x1, waiting for transfers between devices, all_blocks(): lax.all_to_all(jnp.stack([parts] * lax.axis_size(axes[k])), axes[k], 0, 0)  87.4 us
    all_gather x1, blocking collectives, side_by_side(): result, at, done = (lax.all_gather(both, axis, axis=dim, tiled=True), 0, [])  52 us
    all_to_all x1, waiting for transfers between devices, per_device(): lax.all_to_all(query_left_factors, POP, split_axis=1, concat_axis=0, tile...  44 us
    all_to_all x1, waiting for transfers between devices, per_device(): lax.all_to_all(o_right, POP, split_axis=2, concat_axis=0, tiled=True)  38.8 us
    all_to_all x2, blocking collectives, all_blocks(): lax.all_to_all(jnp.stack([parts] * lax.axis_size(axes[k])), axes[k], 0, 0)  22.9 us
    all_to_all x1, waiting for transfers between devices, summed_on_arrival(): lax.all_to_all(cut_along(shard, dim, devices), axis, 0, 0, tiled=True)  22.5 us
    all_to_all x2, starting transfers between devices, copy_for_each(): return lax.all_to_all(copies, axis, split_axis=0, concat_axis=0, tiled=True)  13.3 us
    unnamed x35, local copies, waits for them, and re-layouts  12 us
  transfers between devices with their start and end apart: 7, of which 5 were waited for; matrix products, arithmetic and copies ran while one was open for 11% of the time, Pallas kernels for 0%

profile of v1, /device:TPU:1, one launch (start us, length us, event | category | flops | bytes accessed | tf_op | source)
XLA Modules:
  0.0 402.6 jit_solution(16368670677369238113)
XLA Ops:
  7.2 0.7 all-gather.3.cloned.1.call-update
  7.9 0.9 stack.9
  8.8 11.9 %all_to_all.62 = bf16[4,1,56,896]{3,2,1,0:T(8,128)(2,1)S(1)} all-to-all(bf16[4,1,56,896]{3,2,1,0:T(8,128)(2,1)S(1)} %stack.9), channel_id=1, replica_groups=mesh['pop_0'=4,'pop_1'=8,'pop_2'=2,'mp'=4] {'pop_0'}, dimensions={0} | all-to-all | bytes 802816 | tf_op jit(solution)/shard_map/all_to_all | solution.py:29
  20.7 1.9 stack.10
  22.6 8.3 %all-to-all-start.2 = ((bf16[8,4,56,896]{3,2,1,0:T(8,128)(2,1)}), bf16[8,4,56,896]{3,2,1,0:T(8,128)(2,1)}, u32[]{:S(2)}, u32[]{:S(2)}) async-start(bf16[8,4,56,896]{3,2,1,0:T(8,128)(2,1)} %stack.10), calls=%async_computation.2 | async-start | bytes 6422528 | tf_op jit(solution)/shard_map/all_to_all | solution.py:29
  31.7 0.7 convolution_bitcast_fusion.1
  32.4 1.0 fusion.18
  33.4 0.5 fusion.13
  33.9 87.4 %all-to-all-done.2 = bf16[8,4,56,896]{3,2,1,0:T(8,128)(2,1)} async-done(((bf16[8,4,56,896]{3,2,1,0:T(8,128)(2,1)}), bf16[8,4,56,896]{3,2,1,0:T(8,128)(2,1)}, u32[]{:S(2)}, u32[]{:S(2)}) %all-to-all-start.2) | async-done | bytes 3211296 | tf_op jit(solution)/shard_map/all_to_all | solution.py:29
  121.3 3.5 pad_maximum_fusion
  124.9 11.0 %all_to_all.63 = bf16[2,32,56,896]{3,2,1,0:T(8,128)(2,1)S(1)} all-to-all(bf16[2,32,56,896]{3,2,1,0:T(8,128)(2,1)S(1)} %pad_maximum_fusion), channel_id=1, replica_groups=mesh['pop_0'=4,'pop_1'=8,'pop_2'=2,'mp'=4] {'pop_2'}, dimensions={0} | all-to-all | bytes 12845056 | tf_op jit(solution)/shard_map/all_to_all | solution.py:29
  135.9 0.5 copy.115
  136.5 2.9 convolution_bitcast_fusion
  139.3 2.2 fusion.3
  141.6 0.9 fusion.27
  142.4 1.3 copy.142
  143.8 1.3 copy.143
  145.0 1.4 fusion.7
  146.5 0.6 fusion.28
  147.1 1.2 copy-done.2
  148.3 0.3 fusion.2
  148.6 0.3 copy-done.13
  148.9 2.6 convolution_convert_fusion
  151.5 0.2 fusion.23
  151.7 5.0 %fusion.29 = f32[256,3584]{1,0:T(8,128)S(1)} fusion(bf16[256,896]{0,1:T(8,128)(2,1)S(1)} %bitcast.109, bf16[896,3584]{0,1:T(8,128)(2,1)} %all-gather.3.cloned.1.call-done), kind=kOutput, calls=%fused_computation.59 | convolution fusion | flops 1644167168 | bytes 10551296 | tf_op jit(solution)/shard_map/mtf,fe->mte/dot_general | solution.py:148
  156.7 3.1 fusion.1
  159.8 3.3 reshape.288
  163.1 1.5 copy.147
  164.6 4.1 %all-to-all-start.4 = ((bf16[4,1,256,896]{3,2,1,0:T(8,128)(2,1)}), bf16[4,1,256,896]{3,2,1,0:T(8,128)(2,1)S(1)}, u32[]{:S(2)}, u32[]{:S(2)}) async-start(bf16[4,1,256,896]{3,2,1,0:T(8,128)(2,1)} %bitcast.101), calls=%async_computation.4 | async-start | bytes 3670016 | tf_op jit(solution)/shard_map/all_to_all | solution.py:48
  168.7 0.2 copy.127
  168.9 0.3 reshape.291
  169.2 22.5 %all-to-all-done.4 = bf16[4,1,256,896]{3,2,1,0:T(8,128)(2,1)S(1)} async-done(((bf16[4,1,256,896]{3,2,1,0:T(8,128)(2,1)}), bf16[4,1,256,896]{3,2,1,0:T(8,128)(2,1)S(1)}, u32[]{:S(2)}, u32[]{:S(2)}) %all-to-all-start.4) | async-done | bytes 1835040 | tf_op jit(solution)/shard_map/all_to_all | solution.py:48
  191.7 0.2 convert_reduce_fusion
  192.0 0.9 multiply_reduce_fusion
  192.8 0.6 broadcast_in_dim.16
  193.5 6.5 %all_to_all.64 = f32[4,1,1]{2,1,0:T(1,128)S(1)} all-to-all(f32[4,1,1]{2,1,0:T(1,128)S(1)} %broadcast_in_dim.16), channel_id=1, replica_groups=mesh['pop_0'=4,'pop_1'=8,'pop_2'=2,'mp'=4] {'mp'}, dimensions={0} | all-to-all | bytes 32 | tf_op jit(solution)/shard_map/all_to_all | solution.py:54
  200.0 0.6 reduce_sum.57
  201.2 0.6 broadcast_in_dim.17
  201.9 7.3 %all-to-all-start.6 = ((f32[64,1,1]{2,1,0:T(1,128)}), f32[64,1,1]{2,1,0:T(1,128)S(1)}, u32[]{:S(2)}, u32[]{:S(2)}) async-start(f32[64,1,1]{2,1,0:T(1,128)} %broadcast_in_dim.17), calls=%async_computation.6 | async-start | bytes 65536 | tf_op jit(solution)/shard_map/all_to_all | solution.py:54
  209.2 52.0 %all-gather = bf16[64,1,7168]{2,1,0:T(2,128)(2,1)S(1)} all-gather(bf16[1,1,7168]{2,1,0:T(2,128)(2,1)S(1)} %maximum_bitcast_fusion.2), channel_id=1, replica_groups=mesh['pop_0'=4,'pop_1'=8,'pop_2'=2,'mp'=4] {'pop_0','pop_1','pop_2'}, dimensions={0}, use_global_device_ids=true | all-gather | bytes 931840 | tf_op jit(solution)/shard_map/all_gather | solution.py:68
  261.2 3.2 copy.130
  264.4 1.2 copy.148
  265.6 7.3 %all-to-all-start.8 = ((bf16[1,4,3584]{1,0,2:T(2,128)(2,1)}), bf16[1,4,3584]{1,0,2:T(2,128)(2,1)S(1)}, u32[]{:S(2)}, u32[]{:S(2)}) async-start(bf16[1,4,3584]{1,0,2:T(2,128)(2,1)} %copy.130), calls=%async_computation.8 | async-start | bytes 3670016 | tf_op jit(solution)/shard_map/all_to_all | solution.py:169
  272.9 2.0 slice_convert_fusion
  275.0 3.2 copy.113
  278.1 0.7 reduce_sum.58
  279.5 38.8 %all-to-all-done.8 = bf16[1,4,3584]{1,0,2:T(2,128)(2,1)S(1)} async-done(((bf16[1,4,3584]{1,0,2:T(2,128)(2,1)}), bf16[1,4,3584]{1,0,2:T(2,128)(2,1)S(1)}, u32[]{:S(2)}, u32[]{:S(2)}) %all-to-all-start.8) | async-done | bytes 28704 | tf_op jit(solution)/shard_map/all_to_all | solution.py:169
  318.3 6.2 %all-to-all-start = ((bf16[1,3584,4]{2,0,1:T(2,128)(2,1)}), bf16[1,3584,4]{2,0,1:T(2,128)(2,1)}, u32[]{:S(2)}, u32[]{:S(2)}) async-start(bf16[1,3584,4]{2,0,1:T(2,128)(2,1)} %copy.113), calls=%async_computation | async-start | bytes 3670016 | tf_op jit(solution)/shard_map/all_to_all | solution.py:168
  324.5 0.6 multiply_reduce_fusion.1
  325.8 44.0 %all-to-all-done = bf16[1,3584,4]{2,0,1:T(2,128)(2,1)} async-done(((bf16[1,3584,4]{2,0,1:T(2,128)(2,1)}), bf16[1,3584,4]{2,0,1:T(2,128)(2,1)}, u32[]{:S(2)}, u32[]{:S(2)}) %all-to-all-start) | async-done | bytes 28704 | tf_op jit(solution)/shard_map/all_to_all | solution.py:168
  369.8 0.6 broadcast_in_dim.32
  370.4 6.0 %all-to-all-start.7 = ((f32[64,1,1]{2,1,0:T(1,128)}), f32[64,1,1]{2,1,0:T(1,128)S(1)}, u32[]{:S(2)}, u32[]{:S(2)}) async-start(f32[64,1,1]{2,1,0:T(1,128)} %broadcast_in_dim.32), calls=%async_computation.7 | async-start | bytes 65536 | tf_op jit(solution)/shard_map/all_to_all | solution.py:54
  376.4 1.8 copy.128
  378.2 1.3 reshape.292
  379.5 1.8 copy.131
  381.6 3.7 copy.114
  385.3 0.1 reshape.295
  385.5 0.2 all-to-all-done.7
  385.7 0.6 reduce.10
  386.2 1.6 multiply_bitcast_fusion
  387.8 2.9 copy.129
  390.7 1.5 reshape.293
  392.4 1.1 convolution_multiply_fusion.3
  393.5 1.1 convolution_multiply_fusion.2
  (38 shorter events, 0.6 us)
Async XLA Ops:
  7.2 24.5 %copy-start = (bf16[256,3584]{1,0:T(8,128)(2,1)S(1)}, bf16[256,3584]{1,0:T(8,128)(2,1)}, u32[]{:S(2)}) copy-start(bf16[256,3584]{1,0:T(8,128)(2,1)} %param.11) | copy-start | bytes 5505028
  7.2 144.5 %all-gather.3.cloned.1.call-start = ((), (), s32[]{:S(2)}) async-start(), calls=%async_computation.9 | async-start | bytes 6522880 | tf_op jit(solution)/shard_map/all_gather | solution.py:151
  22.6 9.0 %copy-start.4 = (bf16[3584,128]{1,0:T(8,128)(2,1)S(1)}, bf16[3584,128]{1,0:T(8,128)(2,1)}, u32[]{:S(2)}) copy-start(bf16[3584,128]{1,0:T(8,128)(2,1)} %param.14) | copy-start | bytes 2752516
  22.6 98.7 %all-to-all-start.2 = ((bf16[8,4,56,896]{3,2,1,0:T(8,128)(2,1)}), bf16[8,4,56,896]{3,2,1,0:T(8,128)(2,1)}, u32[]{:S(2)}, u32[]{:S(2)}) async-start(bf16[8,4,56,896]{3,2,1,0:T(8,128)(2,1)} %stack.10), calls=%async_computation.2 | async-start | bytes 6422528 | tf_op jit(solution)/shard_map/all_to_all | solution.py:29
  136.4 2.9 copy-start.9
  136.4 2.9 copy-start.11
  145.0 1.4 copy-start.6
  145.0 1.4 copy-start.7
  147.1 1.3 copy-start.2
  147.1 1.8 copy-start.13
  148.9 2.6 copy-start.12
  151.7 5.0 %copy-start.8 = (bf16[1,4,3584]{2,1,0:T(4,128)(2,1)S(1)}, bf16[1,4,3584]{2,1,0:T(4,128)(2,1)}, u32[]{:S(2)}) copy-start(bf16[1,4,3584]{2,1,0:T(4,128)(2,1)} %param.20) | copy-start | bytes 86020
  164.6 27.1 %all-to-all-start.4 = ((bf16[4,1,256,896]{3,2,1,0:T(8,128)(2,1)}), bf16[4,1,256,896]{3,2,1,0:T(8,128)(2,1)S(1)}, u32[]{:S(2)}, u32[]{:S(2)}) async-start(bf16[4,1,256,896]{3,2,1,0:T(8,128)(2,1)} %bitcast.101), calls=%async_computation.4 | async-start | bytes 3670016 | tf_op jit(solution)/shard_map/all_to_all | solution.py:48
  168.7 23.3 %copy-start.5 = (bf16[256,896]{1,0:T(8,128)(2,1)S(1)}, bf16[256,896]{1,0:T(8,128)(2,1)}, u32[]{:S(2)}) copy-start(bf16[256,896]{1,0:T(8,128)(2,1)} %param.12) | copy-start | bytes 1376260
  201.9 63.7 %all-to-all-start.6 = ((f32[64,1,1]{2,1,0:T(1,128)}), f32[64,1,1]{2,1,0:T(1,128)S(1)}, u32[]{:S(2)}, u32[]{:S(2)}) async-start(f32[64,1,1]{2,1,0:T(1,128)} %broadcast_in_dim.17), calls=%async_computation.6 | async-start | bytes 65536 | tf_op jit(solution)/shard_map/all_to_all | solution.py:54
  265.6 52.7 %all-to-all-start.8 = ((bf16[1,4,3584]{1,0,2:T(2,128)(2,1)}), bf16[1,4,3584]{1,0,2:T(2,128)(2,1)S(1)}, u32[]{:S(2)}, u32[]{:S(2)}) async-start(bf16[1,4,3584]{1,0,2:T(2,128)(2,1)} %copy.130), calls=%async_computation.8 | async-start | bytes 3670016 | tf_op jit(solution)/shard_map/all_to_all | solution.py:169
  272.9 2.0 copy-start.10
  318.3 51.5 %all-to-all-start = ((bf16[1,3584,4]{2,0,1:T(2,128)(2,1)}), bf16[1,3584,4]{2,0,1:T(2,128)(2,1)}, u32[]{:S(2)}, u32[]{:S(2)}) async-start(bf16[1,3584,4]{2,0,1:T(2,128)(2,1)} %copy.113), calls=%async_computation | async-start | bytes 3670016 | tf_op jit(solution)/shard_map/all_to_all | solution.py:168
  370.4 15.3 %all-to-all-start.7 = ((f32[64,1,1]{2,1,0:T(1,128)}), f32[64,1,1]{2,1,0:T(1,128)S(1)}, u32[]{:S(2)}, u32[]{:S(2)}) async-start(f32[64,1,1]{2,1,0:T(1,128)} %broadcast_in_dim.32), calls=%async_computation.7 | async-start | bytes 65536 | tf_op jit(solution)/shard_map/all_to_all | solution.py:54
  381.4 4.9 %copy-start.3 = (f32[64,3584]{0,1:T(8,128)S(1)}, f32[64,3584]{0,1:T(8,128)}, u32[]{:S(2)}) copy-start(f32[64,3584]{0,1:T(8,128)} %copy.128) | copy-start | bytes 2752516
  387.8 6.8 %copy-start.1 = (bf16[256,3584]{1,0:T(8,128)(2,1)S(1)}, bf16[256,3584]{1,0:T(8,128)(2,1)}, u32[]{:S(2)}) copy-start(bf16[256,3584]{1,0:T(8,128)(2,1)} %param.11) | copy-start | bytes 5505028
Sparse Core Ops, SparseCore 0:
  10.7 111.3 all-gather.2
